TPU v7x, 256 devices: a 4x2x16 block of a 4x16x16 slice. The times are simulated.
256 devices in a mesh: group: 2 (over y), ctx: 32 (over z, core), exp: 4 (over x).
Axes of the slice: x: 4, y: 2, z: 16, core: 2. Of those that a mesh axis runs over, the one named last changes fastest.
The devices are a block of a 4x16x16 slice.
Arguments:
- queries: bfloat16 [4096, 4096], P(('group', 'ctx'), 'exp'), parts along dimension 0, may hold values from -6 to 6
- new_keys: bfloat16 [4096, 1024], P(('group', 'ctx'), 'exp'), parts along dimension 0, may hold values from -6 to 6
- new_values: bfloat16 [4096, 1024], P(('group', 'ctx'), 'exp'), parts along dimension 0, may hold values from -6 to 6
- cache_keys: bfloat16 [16384, 1024], P(('group', 'ctx'), 'exp'), parts along dimension 0, may hold values from -6 to 6
- cache_values: bfloat16 [16384, 1024], P(('group', 'ctx'), 'exp'), parts along dimension 0, may hold values from -6 to 6
- offset: int32 [2], P('group'), parts along dimension 0, may hold values from 4096 to 8192
- token_ids: int32 [4096], P(('group', 'ctx')), parts along dimension 0, may hold values from 0 to 128255, as said below
- expert_table: int32 [256512], P('group'), parts along dimension 0, may hold values from 0 to 3
- norm_gain: float32 [4096], replicated, may hold values from 0.5 to 1.5
- w_gate: bfloat16 [4, 4096, 14336], P('exp', None, 'ctx'), may hold values from -0.09375 to 0.09375
- w_up: bfloat16 [4, 4096, 14336], P('exp', None, 'ctx'), may hold values from -0.09375 to 0.09375
- w_down: bfloat16 [4, 14336, 4096], P('exp', 'ctx'), may hold values from -0.046875 to 0.046875
Outputs:
- mixed: bfloat16 [4096, 4096], P(('group', 'ctx'), 'exp'), parts along dimension 0
There are 2 independent parts, one for each index of `group`. A program takes and returns all parts, laid end to end along the dimension named above; an argument that names none is the same for every part. Nothing has to cross between parts.
Inputs may be any that keep to these rules, and one draw needn't show every extreme that they name: Cache positions at or beyond offset are not yet filled. `token_ids`: in every block of 64 consecutive stretch tokens (one block per index of ctx) at most 32 tokens map to one expert through expert_table, and one expert takes exactly 32 tokens of every block.
All inputs are finite; a program needn't handle non-finite values.
Results may differ from a plain program's by a relative error of at most 0.025.
Values may be sent and summed in bfloat16 or wider, within the bound.
A program may use at most 128 MiB of HBM per device.

v0:
```python
import math
import jax
import jax.numpy as jnp
from jax import lax
from jax.sharding import Mesh
from jax.sharding import PartitionSpec as P

HEADS = 32
KV_HEADS = 8
HEAD_DIM = 128
CTX = ("ctx_0", "ctx_1")
GROUP_CTX = ("group", "ctx_0", "ctx_1")
masked_score = -1e30


def sent_together(arrays, axis, dim, along):
    widths = [a.shape[along] for a in arrays]
    both = jnp.concatenate(arrays, axis=along)
    filled = lax.all_gather(both, axis, axis=dim, tiled=True)
    return tuple(jnp.split(filled, [sum(widths[:k]) for k in range(1, len(widths))], axis=along))


def own_block(tiles, axes, order):
    shape = [lax.axis_size(a) for a in axes]
    tiles = tiles.reshape(*shape, *tiles.shape[1:])
    tiles = tiles.transpose(*order, *range(len(axes), tiles.ndim))
    tiles = tiles.reshape(-1, *tiles.shape[len(axes) :])
    for k in order:
        tiles = lax.psum_scatter(tiles, axes[k], scatter_dimension=0, tiled=True)
    return tiles[0]


def in_blocks(array, dim, devices):
    shape = array.shape
    tiles = array.reshape(*shape[:dim], devices, shape[dim] // devices, *shape[dim + 1 :])
    return jnp.moveaxis(tiles, dim, 0)


def summed_rows(array, axes, order, dim):
    devices = lax.axis_size(axes)
    return own_block(in_blocks(array, dim, devices), axes, order)


def split_heads(flat, heads):
    return flat.reshape(flat.shape[0], heads, flat.shape[1] // heads)


def partial_attend(query_rows, key_rows, value_rows, allowed):
    width = query_rows.shape[3]
    scores = jnp.einsum("rkgd,skd->rkgs", query_rows, key_rows, preferred_element_type=jnp.float32)
    scores = scores * (1.0 / math.sqrt(width))
    usable = allowed[:, None, None, :]
    peak = jnp.max(jnp.where(usable, scores, masked_score), axis=-1)
    unnorm = jnp.where(usable, jnp.exp(scores - peak[..., None]), 0.0)
    total = jnp.sum(unnorm, axis=-1)
    numer = jnp.einsum(
        "rkgs,skd->rkgd",
        unnorm.astype(jnp.bfloat16),
        value_rows,
        preferred_element_type=jnp.float32,
    )
    return (numer, peak, total)


def on_device(
    queries,
    new_keys,
    new_values,
    cache_keys,
    cache_values,
    offset,
    token_ids,
    expert_table,
    norm_gain,
    w_gate,
    w_up,
    w_down,
):
    owners = lax.axis_size("exp")
    heads_local = HEADS // owners
    kv_local = KV_HEADS // owners
    group = HEADS // KV_HEADS
    tok_count = queries.shape[0]
    cache_len = cache_keys.shape[0]
    shard = lax.axis_index(CTX)
    limit = offset[0]
    key_rows = jnp.concatenate([cache_keys, new_keys], axis=0)
    value_rows = jnp.concatenate([cache_values, new_values], axis=0)
    span = key_rows.shape[0]
    own_index = shard * tok_count + jnp.arange(tok_count, dtype=jnp.int32)
    grouped = queries.reshape(tok_count, kv_local, group, HEAD_DIM)
    piece_keys, piece_values = sent_together((key_rows, value_rows), CTX, 0, 1)
    flat = jnp.arange(piece_keys.shape[0], dtype=jnp.int32)
    source = flat // span
    inner = flat % span
    cache_ok = source * cache_len + inner < limit
    stretch_ok = (source * tok_count + inner - cache_len)[None, :] <= own_index[:, None]
    allowed = jnp.where((inner < cache_len)[None, :], cache_ok[None, :], stretch_ok)
    numer, peak, total = partial_attend(
        grouped, split_heads(piece_keys, kv_local), split_heads(piece_values, kv_local), allowed
    )
    best = jnp.full((tok_count, kv_local, group), masked_score, jnp.float32)
    higher = jnp.maximum(best, peak)
    fresh = jnp.exp(peak - higher)
    accum = numer * fresh[..., None]
    denom = total * fresh
    attended = (
        (accum / denom[..., None]).reshape(tok_count, heads_local * HEAD_DIM).astype(jnp.bfloat16)
    )
    capacity = tok_count // 2
    chosen = expert_table[token_ids]
    onehot = (chosen[:, None] == jnp.arange(owners, dtype=jnp.int32)[None, :]).astype(jnp.int32)
    earlier = jnp.cumsum(onehot, axis=0) - onehot
    slot = jnp.sum(earlier * onehot, axis=1)
    target = chosen * capacity + slot
    dispatch = (jnp.arange(owners * capacity, dtype=jnp.int32)[:, None] == target[None, :]).astype(
        jnp.bfloat16
    )
    packed = jnp.dot(dispatch, attended, preferred_element_type=jnp.float32).astype(jnp.bfloat16)
    arrived = lax.all_to_all(packed, "exp", split_axis=0, concat_axis=1, tiled=True)
    values32 = arrived.astype(jnp.float32)
    scale = lax.rsqrt(jnp.mean(values32 * values32, axis=-1, keepdims=True) + 1e-05)
    normed = (values32 * scale * norm_gain).astype(jnp.bfloat16)
    gate_w = w_gate[0]
    up_w = w_up[0]
    down_w = w_down[0]
    piece = lax.all_gather(normed, CTX, axis=0, tiled=True)
    gate = jnp.dot(piece, gate_w, preferred_element_type=jnp.float32)
    upper = jnp.dot(piece, up_w, preferred_element_type=jnp.float32)
    hidden = (jax.nn.silu(gate) * upper).astype(jnp.bfloat16)
    summed = summed_rows(
        jnp.dot(hidden, down_w, preferred_element_type=jnp.float32).astype(jnp.bfloat16),
        CTX,
        (1, 0),
        0,
    ).astype(jnp.float32)
    combined = (normed.astype(jnp.float32) + summed).astype(jnp.bfloat16)
    returned = lax.all_to_all(combined, "exp", split_axis=1, concat_axis=0, tiled=True)
    collect = (target[:, None] == jnp.arange(owners * capacity, dtype=jnp.int32)[None, :]).astype(
        jnp.bfloat16
    )
    return jnp.dot(collect, returned, preferred_element_type=jnp.float32).astype(jnp.bfloat16)


def solution(mesh):
    torus = Mesh(
        mesh.devices.reshape(mesh.shape["group"], 16, 2, mesh.shape["exp"]),
        ("group", "ctx_0", "ctx_1", "exp"),
    )
    placed = (
        P(GROUP_CTX, "exp"),
        P(GROUP_CTX, "exp"),
        P(GROUP_CTX, "exp"),
        P(GROUP_CTX, "exp"),
        P(GROUP_CTX, "exp"),
        P("group"),
        P(GROUP_CTX),
        P("group"),
        P(),
        P("exp", None, CTX),
        P("exp", None, CTX),
        P("exp", CTX, None),
    )
    return jax.shard_map(
        on_device, mesh=torus, in_specs=placed, out_specs=P(GROUP_CTX, "exp"), check_vma=False
    )
```

profile of v0, /device:TPU:40, one launch (start us, length us, event | category | flops | bytes accessed | tf_op | source)
XLA Modules:
  0.0 400.0 jit_solution(10660511344860597699)
XLA Ops:
  6.5 0.0 copy-start
  6.6 0.0 all-gather.3.cloned.1.call-start
  6.6 1.8 maximum_maximum_fusion
  8.4 0.1 all-gather.3.cloned.1.call-update
  8.4 0.1 all-gather.5.cloned.1.call-start
  9.2 1.0 reshape.150
  10.1 0.7 compare_select_fusion.1
  10.8 0.0 copy-done
  10.8 0.8 gather_fusion
  11.6 0.1 fusion.40
  11.7 0.1 reduce_window_sum.11
  11.8 0.2 select_reduce_fusion
  12.0 0.5 compare_select_fusion
  12.6 89.4 %all-gather.3.cloned.1.call-done = bf16[10240,512]{1,0:T(8,128)(2,1)} async-done(((bf16[320,512]{1,0:T(8,128)(2,1)}), bf16[10240,512]{1,0:T(8,128)(2,1)}) %all-gather.3.cloned.1.call-update) | async-done | bytes 10485776 | tf_op jit(solution)/shard_map/all_gather | solution.py:19
  102.0 8.9 %fusion.47 = (bf16[10240,256]{1,0:T(8,128)(2,1)}, bf16[10240,256]{1,0:T(8,128)(2,1)}) fusion(bf16[10240,512]{1,0:T(8,128)(2,1)} %all-gather.3.cloned.1.call-done), kind=kLoop, calls=%fused_computation.65 | loop fusion | bytes 20971520 | tf_op jit(solution)/shard_map/split | solution.py:20
  110.9 7.9 %copy.50 = bf16[10240,256]{0,1:T(8,128)(2,1)} copy(bf16[10240,256]{1,0:T(8,128)(2,1)} %get-tuple-element.6) | data formatting | bytes 10485760
  118.8 8.0 %copy.51 = bf16[10240,256]{0,1:T(8,128)(2,1)} copy(bf16[10240,256]{1,0:T(8,128)(2,1)} %get-tuple-element.5) | data formatting | bytes 10485760
  126.7 12.0 %fusion = (f32[64,2,4]{0,2,1:T(4,128)S(1)}, f32[2,10240,64,4]{1,2,3,0:T(8,128)}) fusion(pred[64,10240]{1,0:T(8,128)(4,1)S(1)} %compare_select_fusion, bf16[10240,2,128,1]{0,2,3,1:T(8,128)(2,1)} %bitcast.77, bf16[64,2,4,128]{3,2,1,0:T(4,128)(2,1)S(1)} %reshape.150), kind=kOutput, calls=%fused_computation.3 | convolution fusion | flops 1357905408 | bytes 27002880 | tf_op jit(solution)/shard_map/rkgd,skd->rkgs/dot_general | solution.py:50
  138.7 10.0 %fusion.3 = f32[64,2,4]{0,2,1:T(4,128)S(1)} fusion(f32[2,10240,64,4]{1,2,3,0:T(8,128)} %get-tuple-element.10, f32[64,2,4]{0,2,1:T(4,128)S(1)} %get-tuple-element.9, pred[64,10240]{1,0:T(8,128)(4,1)S(1)} %compare_select_fusion), kind=kLoop, calls=%fused_computation.6 | loop fusion | flops 20971008 | bytes 21630976 | tf_op jit(solution)/shard_map/reduce_sum | solution.py:55
  148.7 0.0 copy-start.2
  148.7 10.6 %fusion.26 = bf16[64,2,4,128]{3,0,2,1:T(8,128)(2,1)S(1)} fusion(bf16[10240,2,128,1]{0,2,3,1:T(8,128)(2,1)} %bitcast.79, f32[2,10240,64,4]{1,2,3,0:T(8,128)} %get-tuple-element.10, f32[64,2,4]{0,2,1:T(4,128)S(1)} %get-tuple-element.9, pred[64,10240]{1,0:T(8,128)(4,1)S(1)} %compare_select_fusion, f32[64,2,4]{0,2,1:T(4,128)S(1)} %get-tuple-element.8, ...), kind=kOutput, calls=%fused_computation.23 | convolution fusion | flops 1363345408 | bytes 27006976 | tf_op jit(solution)/shard_map/rkgs,skd->rkgd/dot_general | solution.py:56
  159.4 0.1 copy.40
  159.5 0.1 convert_element_type.62
  159.6 0.2 convolution_convert_fusion.1
  159.8 11.1 %all_to_all.29 = bf16[4,32,1024]{2,1,0:T(8,128)(2,1)S(1)} all-to-all(bf16[4,32,1024]{2,1,0:T(8,128)(2,1)S(1)} %bitcast.83), channel_id=1, replica_groups=mesh['group'=2,'ctx_0'=16,'ctx_1'=2,'exp'=4] {'exp'}, dimensions={0} | all-to-all | bytes 524288 | tf_op jit(solution)/shard_map/all_to_all | solution.py:120
  170.9 0.2 copy_convert_fusion
  171.1 0.3 copy.52
  171.4 0.4 multiply_reduce_fusion
  171.8 0.0 copy-done.2
  171.8 0.8 multiply_convert_fusion.1
  172.6 0.1 all-gather.5.cloned.1.call-update
  172.7 0.2 reduce-scatter.3.cloned.1.call-start
  172.9 71.4 %all-gather.5.cloned.1.call-done = bf16[1024,4096]{1,0:T(8,128)(2,1)} async-done(((bf16[32,4096]{1,0:T(8,128)(2,1)}), bf16[1024,4096]{1,0:T(8,128)(2,1)}) %all-gather.5.cloned.1.call-update) | async-done | bytes 8388624 | tf_op jit(solution)/shard_map/all_gather | solution.py:127
  244.3 7.5 %fusion.11 = f32[1024,448]{0,1:T(8,128)S(1)} fusion(bf16[1024,4096]{1,0:T(8,128)(2,1)} %all-gather.5.cloned.1.call-done, bf16[1,4096,448]{1,2,0:T(8,128)(2,1)} %param.21), kind=kOutput, calls=%fused_computation.14 | convolution fusion | flops 3758096384 | bytes 13893632 | tf_op jit(solution)/shard_map/dot_general | solution.py:128
  251.8 15.2 %convolution_convert_fusion = bf16[1024,4096]{1,0:T(8,128)(2,1)} fusion(bf16[1,448,4096]{2,1,0:T(8,128)(2,1)} %param.23, f32[1024,448]{0,1:T(8,128)S(1)} %fusion.11, bf16[1024,4096]{1,0:T(8,128)(2,1)} %all-gather.5.cloned.1.call-done, bf16[1,4096,448]{1,2,0:T(8,128)(2,1)} %param.22), kind=kOutput, calls=%fused_computation.10 | convolution fusion | flops 7523139584 | bytes 25952256 | tf_op jit(solution)/shard_map/dot_general | solution.py:132
  267.0 7.7 %copy.42 = bf16[16,2,32,4096]{3,2,0,1:T(8,128)(2,1)} copy(bf16[16,2,32,4096]{3,2,1,0:T(8,128)(2,1)} %bitcast.78) | data formatting | bytes 16777216 | tf_op jit(solution)/shard_map/reshape;reshape | solution.py:25
  274.8 0.1 reduce-scatter.3.cloned.1.call-update
  274.8 0.0 copy-start.1
  274.8 0.1 reduce-scatter.5.cloned.1.call-start
  274.9 22.1 %reduce-scatter.3.cloned.1.call-done = bf16[16,32,4096]{2,1,0:T(8,128)(2,1)} async-done(((bf16[32,32,4096]{2,1,0:T(8,128)(2,1)}), bf16[16,32,4096]{2,1,0:T(8,128)(2,1)}) %reduce-scatter.3.cloned.1.call-update) | async-done | bytes 4194320 | tf_op jit(solution)/shard_map/reduce_scatter | solution.py:29
  297.0 0.1 reduce-scatter.5.cloned.1.call-update
  297.1 82.6 %reduce-scatter.5.cloned.1.call-done = bf16[1,32,4096]{2,1,0:T(8,128)(2,1)} async-done(((bf16[16,32,4096]{2,1,0:T(8,128)(2,1)}), bf16[1,32,4096]{2,1,0:T(8,128)(2,1)}) %reduce-scatter.5.cloned.1.call-update) | async-done | bytes 262160 | tf_op jit(solution)/shard_map/reduce_scatter | solution.py:29
  379.7 1.4 reshape.153
  381.1 0.3 fusion.30
  381.4 0.1 copy.43
  381.4 11.2 %all_to_all.30 = bf16[32,4,1024]{2,0,1:T(8,128)(2,1)S(1)} all-to-all(bf16[32,4,1024]{2,0,1:T(8,128)(2,1)S(1)} %copy.43), channel_id=1, replica_groups=mesh['group'=2,'ctx_0'=16,'ctx_1'=2,'exp'=4] {'exp'}, dimensions={1} | all-to-all | bytes 524288 | tf_op jit(solution)/shard_map/all_to_all | solution.py:138
  392.6 0.9 convolution_convert_fusion.2
  393.5 0.0 copy-done.1
  (8 shorter events, 0.1 us)
Async XLA Ops:
  6.5 4.3 %copy-start = (s32[128256]{0:T(1024)S(1)}, s32[128256]{0:T(1024)}, u32[]{:S(2)}) copy-start(s32[128256]{0:T(1024)} %param.19) | copy-start | bytes 1539076
  6.6 95.5 %all-gather.3.cloned.1.call-start = ((), (), s32[]{:S(2)}) async-start(), calls=%async_computation.4 | async-start | bytes 10813440 | tf_op jit(solution)/shard_map/all_gather | solution.py:19
  8.4 235.9 %all-gather.5.cloned.1.call-start = ((), (), s32[]{:S(2)}) async-start(), calls=%async_computation.5 | async-start | bytes 8650752 | tf_op jit(solution)/shard_map/all_gather | solution.py:127
  148.7 23.0 %copy-start.2 = (f32[4096]{0:T(1024)S(1)}, f32[4096]{0:T(1024)}, u32[]{:S(2)}) copy-start(f32[4096]{0:T(1024)} %param.20) | copy-start | bytes 49156
  172.7 124.3 %reduce-scatter.3.cloned.1.call-start = ((), (), s32[]{:S(2)}) async-start(), calls=%async_computation.6 | async-start | bytes 12582912 | tf_op jit(solution)/shard_map/reduce_scatter | solution.py:29
  274.8 118.7 %copy-start.1 = (s32[128256]{0:T(1024)S(1)}, s32[128256]{0:T(1024)}, u32[]{:S(2)}) copy-start(s32[128256]{0:T(1024)} %param.19) | copy-start | bytes 1539076
  274.8 104.9 %reduce-scatter.5.cloned.1.call-start = ((), (), s32[]{:S(2)}) async-start(), calls=%async_computation.7 | async-start | bytes 4456448 | tf_op jit(solution)/shard_map/reduce_scatter | solution.py:29
Sparse Core Ops, SparseCore 0:
  9.2 92.7 all-gather.2
  172.8 71.4 all-gather.4
  274.9 22.0 reduce-scatter.2
  299.4 80.2 reduce-scatter.4
where the time goes:
time: 401 us; the launch traced here: 400 us
  waiting for transfers between devices  266 us (66%)
  matrix products  46.4 us (12%)
  local copies, waits for them, and re-layouts  36.1 us (9%)
  blocking collectives  22.3 us (6%)
  other arithmetic  15.2 us (4%)
  between operations  13.9 us (3%)
    reduce_scatter x2, waiting for transfers between devices, own_block(): tiles = lax.psum_scatter(tiles, axes[k], scatter_dimension=0, tiled=True)  105 us
    all_gather x1, waiting for transfers between devices, sent_together(): filled = lax.all_gather(both, axis, axis=dim, tiled=True)  89.4 us
    all_gather x1, waiting for transfers between devices, on_device(): piece = lax.all_gather(normed, CTX, axis=0, tiled=True)  71.4 us
    unnamed x9, local copies, waits for them, and re-layouts  16.2 us
    dot_general x1, matrix products, on_device(): jnp.dot(hidden, down_w, preferred_element_type=jnp.float32)  15.2 us
    dot_general x1, matrix products, partial_attend(): jnp.einsum('rkgd,skd->rkgs', query_rows, key_rows, preferred_element_type...  12 us
    all_to_all x1, blocking collectives, on_device(): lax.all_to_all(combined, 'exp', split_axis=1, concat_axis=0, tiled=True)  11.2 us
    all_to_all x1, blocking collectives, on_device(): lax.all_to_all(packed, 'exp', split_axis=0, concat_axis=1, tiled=True)  11.1 us
  transfers between devices with their start and end apart: 4, of which 4 were waited for; matrix products, arithmetic and copies ran while one was open for 1% of the time, Pallas kernels for 0%

commit v1 on v0

--- a/solution.py
+++ b/solution.py
@@ -4,6 +4,7 @@
 from jax import lax
 from jax.sharding import Mesh
 from jax.sharding import PartitionSpec as P
+from jax.lax import all_to_all, axis_size
 
 HEADS = 32
 KV_HEADS = 8
@@ -76,6 +77,15 @@
     w_up,
     w_down,
 ):
+
+    def set_meet(mine_x):
+        return jnp.concatenate(
+            all_to_all(
+                jnp.stack([mine_x] * axis_size(CTX)), axis_name=CTX, split_axis=0, concat_axis=0
+            ),
+            axis=0,
+        )
+
     owners = lax.axis_size("exp")
     heads_local = HEADS // owners
     kv_local = KV_HEADS // owners
@@ -124,7 +134,7 @@
     gate_w = w_gate[0]
     up_w = w_up[0]
     down_w = w_down[0]
-    piece = lax.all_gather(normed, CTX, axis=0, tiled=True)
+    piece = set_meet(normed)
     gate = jnp.dot(piece, gate_w, preferred_element_type=jnp.float32)
     upper = jnp.dot(piece, up_w, preferred_element_type=jnp.float32)
     hidden = (jax.nn.silu(gate) * upper).astype(jnp.bfloat16)

time: 401 us -> 701 us (1.75)
  blocking collectives: 22.3 us -> 401 us
  waiting for transfers between devices: 266 us -> 188 us
    all_to_all x0 -> x1, blocking collectives: none -> 378 us  [set_meet(): all_to_all(jnp.stack([mine_x] * axis_size(CTX)), axis_name=CTX, split_axi...]
    all_gather x1 -> x0, waiting for transfers between devices: 71.4 us -> none  [on_device(): piece = lax.all_gather(normed, CTX, axis=0, tiled=True)]
    unnamed x9 -> x13, local copies, waits for them, and re-layouts: 16.2 us -> 19.4 us
  transfers between devices with their start and end apart: 4 -> 3, of which waited for: 4 -> 3; matrix products, arithmetic and copies ran while one was open for 1% -> 0% of each run, Pallas kernels for 0% -> 0%
where the time goes in v1:
time: 701 us; the launch traced here: 700 us
  blocking collectives  401 us (57%)
  waiting for transfers between devices  188 us (27%)
  matrix products  42.9 us (6%)
  local copies, waits for them, and re-layouts  40.4 us (6%)
  other arithmetic  14.5 us (2%)
  between operations  13.9 us (2%)
    all_to_all x1, blocking collectives, set_meet(): all_to_all(jnp.stack([mine_x] * axis_size(CTX)), axis_name=CTX, split_axi...  378 us
    reduce_scatter x2, waiting for transfers between devices, own_block(): tiles = lax.psum_scatter(tiles, axes[k], scatter_dimension=0, tiled=True)  98 us
    all_gather x1, waiting for transfers between devices, sent_together(): filled = lax.all_gather(both, axis, axis=dim, tiled=True)  89.4 us
    unnamed x13, local copies, waits for them, and re-layouts  19.4 us
    dot_general x1, matrix products, on_device(): jnp.dot(hidden, down_w, preferred_element_type=jnp.float32)  15.2 us
  transfers between devices with their start and end apart: 3, of which 3 were waited for; matrix products, arithmetic and copies ran while one was open for 0% of the time, Pallas kernels for 0%

profile of v1, /device:TPU:40, one launch (start us, length us, event | category | flops | bytes accessed | tf_op | source)
XLA Modules:
  0.0 700.0 jit_solution(10354800393402841174)
XLA Ops:
  6.5 0.0 copy-start
  6.6 0.0 all-gather.2.cloned.1.call-start
  6.6 1.8 maximum_maximum_fusion
  8.4 0.1 all-gather.2.cloned.1.call-update
  8.4 0.1 reduce-scatter.3.cloned.1.call-start
  9.2 1.0 reshape.170
  10.1 0.7 compare_select_fusion.1
  10.8 0.0 copy-done
  10.8 0.8 gather_fusion
  11.6 0.1 fusion.40
  11.7 0.1 reduce_window_sum.11
  11.8 0.2 select_reduce_fusion
  12.0 0.5 compare_select_fusion
  12.6 89.4 %all-gather.2.cloned.1.call-done = bf16[10240,512]{1,0:T(8,128)(2,1)} async-done(((bf16[320,512]{1,0:T(8,128)(2,1)}), bf16[10240,512]{1,0:T(8,128)(2,1)}) %all-gather.2.cloned.1.call-update) | async-done | bytes 10485776 | tf_op jit(solution)/shard_map/all_gather | solution.py:20
  102.0 8.9 %fusion.47 = (bf16[10240,256]{1,0:T(8,128)(2,1)}, bf16[10240,256]{1,0:T(8,128)(2,1)}) fusion(bf16[10240,512]{1,0:T(8,128)(2,1)} %all-gather.2.cloned.1.call-done), kind=kLoop, calls=%fused_computation.65 | loop fusion | bytes 20971520 | tf_op jit(solution)/shard_map/split | solution.py:21
  110.9 7.9 %copy.50 = bf16[10240,256]{0,1:T(8,128)(2,1)} copy(bf16[10240,256]{1,0:T(8,128)(2,1)} %get-tuple-element.6) | data formatting | bytes 10485760
  118.8 8.0 %copy.51 = bf16[10240,256]{0,1:T(8,128)(2,1)} copy(bf16[10240,256]{1,0:T(8,128)(2,1)} %get-tuple-element.5) | data formatting | bytes 10485760
  126.7 12.0 %fusion = (f32[64,2,4]{0,2,1:T(4,128)S(1)}, f32[2,10240,64,4]{1,2,3,0:T(8,128)}) fusion(pred[64,10240]{1,0:T(8,128)(4,1)S(1)} %compare_select_fusion, bf16[10240,2,128,1]{0,2,3,1:T(8,128)(2,1)} %bitcast.78, bf16[64,2,4,128]{3,2,1,0:T(4,128)(2,1)S(1)} %reshape.170), kind=kOutput, calls=%fused_computation.3 | convolution fusion | flops 1357905408 | bytes 27002880 | tf_op jit(solution)/shard_map/rkgd,skd->rkgs/dot_general | solution.py:51
  138.7 10.0 %fusion.3 = f32[64,2,4]{0,2,1:T(4,128)S(1)} fusion(f32[2,10240,64,4]{1,2,3,0:T(8,128)} %get-tuple-element.10, f32[64,2,4]{0,2,1:T(4,128)S(1)} %get-tuple-element.9, pred[64,10240]{1,0:T(8,128)(4,1)S(1)} %compare_select_fusion), kind=kLoop, calls=%fused_computation.6 | loop fusion | flops 20971008 | bytes 21630976 | tf_op jit(solution)/shard_map/reduce_sum | solution.py:56
  148.7 0.0 copy-start.3
  148.7 10.6 %fusion.26 = bf16[64,2,4,128]{3,0,2,1:T(8,128)(2,1)S(1)} fusion(bf16[10240,2,128,1]{0,2,3,1:T(8,128)(2,1)} %bitcast.82, f32[2,10240,64,4]{1,2,3,0:T(8,128)} %get-tuple-element.10, f32[64,2,4]{0,2,1:T(4,128)S(1)} %get-tuple-element.9, pred[64,10240]{1,0:T(8,128)(4,1)S(1)} %compare_select_fusion, f32[64,2,4]{0,2,1:T(4,128)S(1)} %get-tuple-element.8, ...), kind=kOutput, calls=%fused_computation.23 | convolution fusion | flops 1363345408 | bytes 27006976 | tf_op jit(solution)/shard_map/rkgs,skd->rkgd/dot_general | solution.py:57
  159.4 0.1 copy.40
  159.5 0.1 convert_element_type.66
  159.6 0.2 convolution_convert_fusion.1
  159.8 11.1 %all_to_all.34 = bf16[4,32,1024]{2,1,0:T(8,128)(2,1)S(1)} all-to-all(bf16[4,32,1024]{2,1,0:T(8,128)(2,1)S(1)} %bitcast.86), channel_id=1, replica_groups=mesh['group'=2,'ctx_0'=16,'ctx_1'=2,'exp'=4] {'exp'}, dimensions={0} | all-to-all | bytes 524288 | tf_op jit(solution)/shard_map/all_to_all | solution.py:130
  170.9 0.2 copy_convert_fusion
  171.1 0.3 copy.52
  171.4 0.4 multiply_reduce_fusion
  171.8 0.0 copy-done.3
  171.8 0.1 multiply_convert_fusion.1
  171.9 1.0 stack.2
  172.9 0.0 copy-start.4
  172.9 378.1 %all_to_all.35 = bf16[32,32,4096]{2,1,0:T(8,128)(2,1)S(1)} all-to-all(bf16[32,32,4096]{2,1,0:T(8,128)(2,1)S(1)} %stack.2), channel_id=1, replica_groups=mesh['group'=2,'ctx_0'=16,'ctx_1'=2,'exp'=4] {'ctx_0','ctx_1'}, dimensions={0} | all-to-all | bytes 16777216 | tf_op jit(solution)/shard_map/all_to_all | solution.py:83
  551.1 3.2 copy-done.2
  554.3 4.0 fusion.11
  558.3 15.2 %convolution_convert_fusion = bf16[1024,4096]{1,0:T(8,128)(2,1)} fusion(bf16[1,448,4096]{2,1,0:T(8,128)(2,1)} %param.23, f32[1024,448]{0,1:T(8,128)S(1)} %fusion.11, bf16[1024,4096]{1,0:T(8,128)(2,1)} %bitcast.80, bf16[1,4096,448]{1,2,0:T(8,128)(2,1)} %param.22), kind=kOutput, calls=%fused_computation.10 | convolution fusion | flops 7523139584 | bytes 25952256 | tf_op jit(solution)/shard_map/dot_general | solution.py:142
  573.5 7.7 %copy.42 = bf16[16,2,32,4096]{3,2,0,1:T(8,128)(2,1)} copy(bf16[16,2,32,4096]{3,2,1,0:T(8,128)(2,1)} %bitcast.81) | data formatting | bytes 16777216 | tf_op jit(solution)/shard_map/reshape;reshape | solution.py:26
  581.2 0.1 reduce-scatter.3.cloned.1.call-update
  581.3 0.0 copy-start.1
  581.3 0.1 reduce-scatter.5.cloned.1.call-start
  581.4 15.4 %reduce-scatter.3.cloned.1.call-done = bf16[16,32,4096]{2,1,0:T(8,128)(2,1)} async-done(((bf16[32,32,4096]{2,1,0:T(8,128)(2,1)}), bf16[16,32,4096]{2,1,0:T(8,128)(2,1)}) %reduce-scatter.3.cloned.1.call-update) | async-done | bytes 4194320 | tf_op jit(solution)/shard_map/reduce_scatter | solution.py:30
  596.8 0.1 reduce-scatter.5.cloned.1.call-update
  596.8 82.6 %reduce-scatter.5.cloned.1.call-done = bf16[1,32,4096]{2,1,0:T(8,128)(2,1)} async-done(((bf16[16,32,4096]{2,1,0:T(8,128)(2,1)}), bf16[1,32,4096]{2,1,0:T(8,128)(2,1)}) %reduce-scatter.5.cloned.1.call-update) | async-done | bytes 262160 | tf_op jit(solution)/shard_map/reduce_scatter | solution.py:30
  679.5 1.4 reshape.174
  680.9 0.3 fusion.30
  681.2 0.1 copy.43
  681.3 11.3 %all_to_all.36 = bf16[32,4,1024]{2,0,1:T(8,128)(2,1)S(1)} all-to-all(bf16[32,4,1024]{2,0,1:T(8,128)(2,1)S(1)} %copy.43), channel_id=1, replica_groups=mesh['group'=2,'ctx_0'=16,'ctx_1'=2,'exp'=4] {'exp'}, dimensions={1} | all-to-all | bytes 524288 | tf_op jit(solution)/shard_map/all_to_all | solution.py:148
  692.6 0.9 convolution_convert_fusion.2
  (11 shorter events, 0.1 us)
Async XLA Ops:
  6.5 4.3 copy-start
  6.6 95.5 %all-gather.2.cloned.1.call-start = ((), (), s32[]{:S(2)}) async-start(), calls=%async_computation.5 | async-start | bytes 10813440 | tf_op jit(solution)/shard_map/all_gather | solution.py:20
  8.4 588.3 %reduce-scatter.3.cloned.1.call-start = ((), (), s32[]{:S(2)}) async-start(), calls=%async_computation.6 | async-start | bytes 12582912 | tf_op jit(solution)/shard_map/reduce_scatter | solution.py:30
  148.7 23.0 %copy-start.3 = (f32[4096]{0:T(1024)S(1)}, f32[4096]{0:T(1024)}, u32[]{:S(2)}) copy-start(f32[4096]{0:T(1024)} %param.20) | copy-start | bytes 49156
  172.9 381.4 %copy-start.4 = (bf16[1,4096,448]{1,2,0:T(8,128)(2,1)S(1)}, bf16[1,4096,448]{1,2,0:T(8,128)(2,1)}, u32[]{:S(2)}) copy-start(bf16[1,4096,448]{1,2,0:T(8,128)(2,1)} %param.21) | copy-start | bytes 11010052
  551.1 3.2 copy-start.2
  581.3 112.2 %copy-start.1 = (s32[128256]{0:T(1024)S(1)}, s32[128256]{0:T(1024)}, u32[]{:S(2)}) copy-start(s32[128256]{0:T(1024)} %param.19) | copy-start | bytes 1539076
  581.3 98.2 %reduce-scatter.5.cloned.1.call-start = ((), (), s32[]{:S(2)}) async-start(), calls=%async_computation.7 | async-start | bytes 4456448 | tf_op jit(solution)/shard_map/reduce_scatter | solution.py:30
Sparse Core Ops, SparseCore 0:
  9.2 92.7 all-gather.1
  581.4 15.3 reduce-scatter.2
  599.3 80.0 reduce-scatter.4
